TPU v7x, 256 devices: a whole 4x4x8 slice. The times are simulated.
256 devices in a mesh: subj: 32 (over x, z_hi, y), vox: 8 (over z_lo, core).
Axes of the slice: x: 4, y: 4, z: 8 (z_hi: 2, z_lo: 4; z = z_hi * 4 + z_lo), core: 2. Of those that a mesh axis runs over, the one named last changes fastest.
Arguments:
- bold_series: float32 [32, 300, 65536], P('subj', None, 'vox')
- seed_index: int32 [256], replicated, may hold values from 0 to 65535
Outputs:
- group_z: float32 [65536, 256], P(('vox', 'subj'))
All inputs are finite; a program needn't handle non-finite values.
Results may differ from a plain program's by a relative error of at most 0.00031.
Values may be sent and summed in bfloat16 or wider, within the bound.
A program may use at most 64 MiB of HBM per device.

v0:
```python
import jax
import jax.numpy as jnp
from jax import lax
from jax.sharding import Mesh
from jax.sharding import PartitionSpec as P

SUBJ = ("subj_0", "subj_1", "subj_2")
VOX_SUBJ = ("vox", "subj_0", "subj_1", "subj_2")


clip_limit = 0.99
epsilon = 1e-05


def from_everyone(shard, axis):
    length = lax.axis_size(axis)
    return lax.all_to_all(
        jnp.broadcast_to(shard[None], (length, *shard.shape)), axis, 0, 0, tiled=True
    )


def of_everyone(shard, axis):
    return from_everyone(shard, axis).astype(jnp.float32).sum(axis=0)


def sum_in_order(parts, axes, order):
    shape = [lax.axis_size(a) for a in axes]
    parts = parts.reshape(*shape, *parts.shape[1:])
    parts = parts.transpose(*order, *range(len(axes), parts.ndim))
    parts = parts.reshape(-1, *parts.shape[len(axes) :])
    for k in order:
        parts = lax.psum_scatter(parts, axes[k], scatter_dimension=0, tiled=True)
    return parts[0]


def split_up(shard, dim, length):
    before, after = (shard.shape[:dim], shard.shape[dim + 1 :])
    return jnp.moveaxis(shard.reshape(*before, length, -1, *after), dim, 0)


def scatter_axes(shard, axes, order, dim):
    length = lax.axis_size(axes)
    return sum_in_order(split_up(shard, dim, length), axes, order)


def normalize(series):
    demean_series = series - jnp.mean(series, axis=0, keepdims=True)
    spread = jnp.mean(demean_series * demean_series, axis=0, keepdims=True)
    return (demean_series * lax.rsqrt(spread + epsilon)).astype(jnp.bfloat16)


def arctanh_transform(cross_product, length):
    clipped = jnp.clip(cross_product * (1.0 / length), -clip_limit, clip_limit)
    return 0.5 * jnp.log((1.0 + clipped) / (1.0 - clipped))


def correlate(normed, seed_panel):
    return lax.dot_general(
        normed, seed_panel, (((0,), (0,)), ((), ())), preferred_element_type=jnp.float32
    )


def body(bold_series, seed_index):
    length = bold_series.shape[1]
    normed = normalize(bold_series[0])
    columns = normed.shape[1]
    groups = lax.axis_size(SUBJ)
    anchor = lax.axis_index("vox") * columns
    offsets = seed_index - anchor
    inside = (offsets >= 0) & (offsets < columns)
    picked = jnp.take(normed, jnp.clip(offsets, 0, columns - 1), axis=1)
    masked = jnp.where(
        inside[None, :], picked.astype(jnp.float32), jnp.zeros(picked.shape, jnp.float32)
    )
    seed_panel = (
        of_everyone(masked.astype(jnp.bfloat16), "vox").astype(jnp.float32).astype(jnp.bfloat16)
    )
    summed = scatter_axes(
        arctanh_transform(correlate(normed, seed_panel), length), SUBJ, (0, 2, 1), 0
    )
    return summed * (1.0 / groups)


def solution(mesh):
    split = Mesh(
        mesh.devices.reshape(4, 2, 4, mesh.shape["vox"]), ("subj_0", "subj_1", "subj_2", "vox")
    )
    placed = (P(SUBJ, None, "vox"), P())
    return jax.shard_map(
        body, mesh=split, in_specs=placed, out_specs=P(VOX_SUBJ, None), check_vma=False
    )
```

profile of v0, /device:TPU:2, one launch (start us, length us, event | category | flops | bytes accessed | tf_op | source)
XLA Modules:
  0.0 259.0 jit_solution(2821266456762475059)
XLA Ops:
  6.5 0.0 reduce-scatter.4.cloned.1.call-start
  6.5 22.2 %copy.9 = f32[1,300,8192]{1,2,0:T(8,128)} copy(f32[1,300,8192]{2,0,1:T(1,128)} %param.2) | data formatting | bytes 19660800 | tf_op args[0]
  28.7 8.8 %reduce_sum.30 = f32[8192]{0:T(1024)S(1)} reduce(f32[1,300,8192]{2,0,1:T(1,128)} %param.2, f32[]{:T(128)} %constant.15.clone.1), dimensions={0,1}, to_apply=%region_0.0 | reduce | flops 2449408 | bytes 9863172 | tf_op jit(solution)/shard_map/reduce_sum | solution.py:47
  37.6 0.0 copy-start
  37.6 7.0 %multiply_reduce_fusion = f32[8192]{0:T(1024)S(1)} fusion(f32[1,300,8192]{1,2,0:T(8,128)} %copy.9, f32[8192]{0:T(1024)S(1)} %broadcast_multiply_fusion), kind=kLoop, calls=%fused_computation.3 | loop fusion | flops 7364608 | bytes 9895936 | tf_op jit(solution)/shard_map/reduce_sum | solution.py:48
  44.6 1.2 copy-done
  45.9 4.2 %multiply_convert_fusion = bf16[300,8192]{0,1:T(8,128)(2,1)} fusion(f32[1,300,8192]{1,2,0:T(8,128)S(1)} %copy-done, f32[8192]{0:T(1024)S(1)} %add_rsqrt_fusion, f32[8192]{0:T(1024)S(1)} %broadcast_multiply_fusion), kind=kLoop, calls=%fused_computation.2 | loop fusion | flops 7372800 | bytes 14811136 | tf_op jit(solution)/shard_map/convert_element_type | solution.py:49
  50.0 4.7 %gather_fusion = bf16[256,300]{1,0:T(8,128)(2,1)S(1)} fusion(bf16[300,8192]{0,1:T(8,128)(2,1)} %multiply_convert_fusion, s32[1024]{0:T(1024)S(1)} %pad_clamp_fusion), kind=kCustom, calls=%fused_computation | custom fusion | bytes 308224 | tf_op jit(solution)/shard_map/jit(_take)/gather | solution.py:71
  54.8 0.1 fusion.1
  54.9 0.1 copy.10
  55.1 0.1 broadcast_in_dim.37
  55.1 36.5 %all_to_all.5 = bf16[8,300,256]{2,1,0:T(8,128)(2,1)S(1)} all-to-all(bf16[8,300,256]{2,1,0:T(8,128)(2,1)S(1)} %broadcast_in_dim.37), channel_id=1, replica_groups=mesh['subj_0'=4,'subj_1'=2,'subj_2'=4,'vox'=8] {'vox'}, dimensions={0} | all-to-all | bytes 2457600 | tf_op jit(solution)/shard_map/all_to_all | solution.py:17
  91.6 0.2 reduce_sum.32
  91.8 5.2 %log_multiply_fusion = f32[8192,256]{1,0:T(8,128)S(1)} fusion(bf16[300,8192]{0,1:T(8,128)(2,1)} %multiply_convert_fusion, bf16[300,256]{1,0:T(8,128)(2,1)S(1)} %reduce_sum.32), kind=kOutput, calls=%fused_computation.6 | convolution fusion | flops 1270874112 | bytes 13457408 | tf_op jit(solution)/shard_map/dot_general | solution.py:58
  97.0 3.8 %copy.12 = f32[4,4,2,256,256]{4,3,2,1,0:T(8,128)} copy(f32[4,4,2,256,256]{4,3,1,2,0:T(8,128)S(1)} %bitcast.17) | data formatting | bytes 16777216 | tf_op jit(solution)/shard_map/transpose | solution.py:29
  100.8 0.0 reduce-scatter.4.cloned.1.call-update
  100.8 0.0 reduce-scatter.6.cloned.1.call-start
  100.8 82.2 %reduce-scatter.4.cloned.1.call-done = f32[8,256,256]{2,1,0:T(8,128)} async-done(((f32[32,256,256]{2,1,0:T(8,128)}), f32[8,256,256]{2,1,0:T(8,128)}) %reduce-scatter.4.cloned.1.call-update) | async-done | bytes 2097168 | tf_op jit(solution)/shard_map/reduce_scatter | solution.py:32
  183.0 0.0 reduce-scatter.6.cloned.1.call-update
  183.1 0.0 reduce-scatter.8.cloned.1.call-start
  183.1 35.8 %reduce-scatter.6.cloned.1.call-done = f32[2,256,256]{2,1,0:T(8,128)} async-done(((f32[8,256,256]{2,1,0:T(8,128)}), f32[2,256,256]{2,1,0:T(8,128)}) %reduce-scatter.6.cloned.1.call-update) | async-done | bytes 524304 | tf_op jit(solution)/shard_map/reduce_scatter | solution.py:32
  218.9 0.0 reduce-scatter.8.cloned.1.call-update
  218.9 31.9 %reduce-scatter.8.cloned.1.call-done = f32[1,256,256]{2,1,0:T(8,128)} async-done(((f32[2,256,256]{2,1,0:T(8,128)}), f32[1,256,256]{2,1,0:T(8,128)}) %reduce-scatter.8.cloned.1.call-update) | async-done | bytes 262160 | tf_op jit(solution)/shard_map/reduce_scatter | solution.py:32
  250.8 1.7 multiply_bitcast_fusion
  (6 shorter events, 0.0 us)
Async XLA Ops:
  6.5 176.5 %reduce-scatter.4.cloned.1.call-start = ((), (), s32[]{:S(2)}) async-start(), calls=%async_computation.4 | async-start | bytes 10485760 | tf_op jit(solution)/shard_map/reduce_scatter | solution.py:32
  37.6 8.3 %copy-start = (f32[1,300,8192]{1,2,0:T(8,128)S(1)}, f32[1,300,8192]{1,2,0:T(8,128)}, u32[]{:S(2)}) copy-start(f32[1,300,8192]{1,2,0:T(8,128)} %copy.9) | copy-start | bytes 29491204
  45.8 4.2 %copy-start.1 = (s32[256]{0:T(256)S(1)}, s32[256]{0:T(256)}, u32[]{:S(2)}) copy-start(s32[256]{0:T(256)} %param.3) | copy-start | bytes 3076
  100.8 118.1 %reduce-scatter.6.cloned.1.call-start = ((), (), s32[]{:S(2)}) async-start(), calls=%async_computation.5 | async-start | bytes 2621440 | tf_op jit(solution)/shard_map/reduce_scatter | solution.py:32
  183.1 67.7 %reduce-scatter.8.cloned.1.call-start = ((), (), s32[]{:S(2)}) async-start(), calls=%async_computation.6 | async-start | bytes 786432 | tf_op jit(solution)/shard_map/reduce_scatter | solution.py:32
Sparse Core Ops, SparseCore 0:
  100.9 82.0 reduce-scatter.3
  185.6 33.2 reduce-scatter.5
  221.4 29.3 reduce-scatter.7
where the time goes:
time: 260 us; the launch traced here: 259 us
  waiting for transfers between devices  150 us (58%)
  blocking collectives  36.5 us (14%)
  local copies, waits for them, and re-layouts  32.2 us (12%)
  other arithmetic  22 us (8%)
  between operations  13.2 us (5%)
  matrix products  5.17 us (2%)
    reduce_scatter x3, waiting for transfers between devices, sum_in_order(): parts = lax.psum_scatter(parts, axes[k], scatter_dimension=0, tiled=True)  150 us
    all_to_all x1, blocking collectives, from_everyone(): lax.all_to_all(jnp.broadcast_to(shard[None], (length, *shard.shape)), axi...  36.5 us
    unnamed x5, local copies, waits for them, and re-layouts  23.4 us
    reduce_sum x1, other arithmetic, normalize(): demean_series = series - jnp.mean(series, axis=0, keepdims=True)  8.82 us
    reduce_sum x1, other arithmetic, normalize(): spread = jnp.mean(demean_series * demean_series, axis=0, keepdims=True)  6.99 us
  transfers between devices with their start and end apart: 3, of which 3 were waited for; matrix products, arithmetic and copies ran while one was open for 0% of the time, Pallas kernels for 0%

commit v1 on v0

v1 whole, which is shorter than its diff:
```python
import functools

import jax
import jax.numpy as jnp
from jax import lax
from jax.experimental import pallas as pl
from jax.experimental.pallas import tpu as pltpu
from jax.sharding import Mesh
from jax.sharding import PartitionSpec as P

AXES = ("x", "zh", "y", "zl", "c")
SUBJ = ("x", "zh", "y")
VOX = ("zl", "c")

CLIP = 0.99
EPS = 1e-05
LIMIT = 2.6466525

T = 300
TP = 320
PIECE = TP // 4
V = 8192
K = 256
TILE = 256
W = 1024
B = 512
H = K // 2
Q = K // 4
SLOTS = 8
SUBJECTS = 32

MESH = pl.DeviceIdType.MESH


def step_of(terms):
    return 32700.0 / (terms * LIMIT) ** 0.5


def encode(z, terms):
    root = z * lax.rsqrt(jnp.maximum(jnp.abs(z), 1e-30))
    return jnp.round(root * step_of(terms)).astype(jnp.int32).astype(jnp.int16)


def decode(q, terms):
    r = q.astype(jnp.int32).astype(jnp.float32)
    return r * jnp.abs(r) * (1.0 / step_of(terms) ** 2)


def fisher(cross):
    c = jnp.clip(cross * (1.0 / T), -CLIP, CLIP)
    return 0.5 * (jnp.log(1.0 + c) - jnp.log(1.0 - c))


def kernel(
    bold, seeds, out,
    raw, normed, acc, panel, pieces, mine, full, seed_t,
    zf, zq, z2, relay, got, s1, s1q, s1m, relay2, got2, s2, s2q, gotz,
    load_sem, rs_send, rs_recv, ag_send, ag_recv,
    a_send, a_recv, b_send, b_recv, z_send, z_recv,
):
    x, zh, y, zl, c = (lax.axis_index(a) for a in AXES)
    xp, xm = lax.rem(x + 1, 4), lax.rem(x + 3, 4)
    yp, ym = lax.rem(y + 1, 4), lax.rem(y + 3, 4)
    peers = [(dz, dc) for dz in range(4) for dc in range(2) if dz or dc]

    def group(dz, dc):
        return {"zl": lax.rem(zl + dz, 4), "c": lax.rem(c + dc, 2)}

    ahead = ({"x": xp}, {"y": yp})
    behind = ({"x": xm}, {"y": ym})
    across = {"zh": 1 - zh}

    barrier = pltpu.get_barrier_semaphore()
    everyone = [group(*p) for p in peers] + [*ahead, *behind, across]
    for other in everyone:
        pl.semaphore_signal(barrier, inc=1, device_id=other, device_id_type=MESH)

    def load(i):
        return pltpu.make_async_copy(
            bold.at[:, 0, pl.ds(pl.multiple_of(i * W, W), W)], raw.at[i], load_sem.at[i]
        )

    @pl.loop(0, V // W)
    def _(i):
        load(i).start()

    acc[...] = jnp.zeros_like(acc)
    anchor = (zl * 2 + c) * V

    @pl.loop(0, V // W)
    def _(i):
        load(i).wait()
        for j in range(W // B):
            series = raw[i, :, j * B : (j + 1) * B]
            center = series - jnp.sum(series, axis=0, keepdims=True) * (1.0 / T)
            spread = jnp.sum(center * center, axis=0, keepdims=True) * (1.0 / T)
            columns = pl.ds(pl.multiple_of(i * W + j * B, B), B)
            normed[pl.ds(T - T % 16, TP - T + T % 16), columns] = jnp.zeros(
                (TP - T + T % 16, B), jnp.bfloat16
            )
            normed[pl.ds(0, T), columns] = (center * lax.rsqrt(spread + EPS)).astype(
                jnp.bfloat16
            )
        ids = lax.broadcasted_iota(jnp.int32, (W, K), 0) + (anchor + i * W)
        chosen = jnp.where(ids == seeds[...], 1.0, 0.0).astype(jnp.bfloat16)
        acc[...] += jnp.dot(
            normed[:, pl.ds(pl.multiple_of(i * W, W), W)],
            chosen,
            preferred_element_type=jnp.float32,
        )

    for h in range(2):
        for p in range(4):
            panel[h, p] = acc[p * PIECE : (p + 1) * PIECE, h * H : (h + 1) * H].astype(
                jnp.bfloat16
            )

    pl.semaphore_wait(barrier, len(everyone))

    def scatter(n):
        to = group(*peers[n])
        return pltpu.make_async_remote_copy(
            src_ref=panel.at[to["c"], to["zl"]],
            dst_ref=pieces.at[n],
            send_sem=rs_send.at[n],
            recv_sem=rs_recv.at[n],
            device_id=to,
            device_id_type=MESH,
        )

    def share(n):
        return pltpu.make_async_remote_copy(
            src_ref=mine,
            dst_ref=full.at[c, zl],
            send_sem=ag_send.at[n],
            recv_sem=ag_recv.at[n],
            device_id=group(*peers[n]),
            device_id_type=MESH,
        )

    def shared(n):
        dz, dc = peers[n]
        return pltpu.make_async_remote_copy(
            src_ref=mine,
            dst_ref=full.at[lax.rem(c + 2 - dc, 2), lax.rem(zl + 4 - dz, 4)],
            send_sem=ag_send.at[n],
            recv_sem=ag_recv.at[n],
            device_id=group(dz, dc),
            device_id_type=MESH,
        )

    for n in range(len(peers)):
        scatter(n).start()
    total = panel[c, zl].astype(jnp.float32)
    for n in range(len(peers)):
        scatter(n).wait_recv()
        total += pieces[n].astype(jnp.float32)
    mine[...] = total.astype(jnp.bfloat16)
    full[c, zl] = mine[...]
    for n in range(len(peers)):
        share(n).start()
    for n in range(len(peers)):
        shared(n).wait_recv()
    for h in range(2):
        whole = jnp.concatenate(
            [full[h, p].astype(jnp.float32) for p in range(4)]
            + [jnp.zeros((384 - TP, H), jnp.float32)],
            axis=0,
        )
        seed_t[h] = whole.T.astype(jnp.bfloat16)
    for n in range(len(peers)):
        scatter(n).wait_send()
        share(n).wait_send()

    def turn(j):
        return lax.rem(2 - j + 3 * (j // 2) + 2 * (j // 3), 4)

    def z_of(h, i, role):
        far = (2, 1, 3, 0)[role]
        g, j = i // 4, lax.rem(i, 4)
        zt = lax.rem(zh + 1 + g, 2)
        if h == 0:
            xt, yt = lax.rem(x + far, 4), lax.rem(y + turn(j), 4)
        else:
            xt, yt = lax.rem(x + turn(j), 4), lax.rem(y + far, 4)
        s = (xt * 2 + zt) * 4 + yt
        columns = pl.ds(pl.multiple_of(s * TILE, TILE), TILE)
        cross = jnp.dot(
            seed_t[h][:, :TP], normed[:, columns], preferred_element_type=jnp.float32
        )
        return fisher(cross)

    def message(i, h, way, kind):
        n = (h * 2 + way) * 3 + kind
        source = z2.at[i, h, way] if kind == 2 else zq.at[i, h, way, kind]
        target = relay.at[i, h, way] if kind == 0 else got.at[i, h, way, kind - 1]
        return pltpu.make_async_remote_copy(
            src_ref=source,
            dst_ref=target,
            send_sem=a_send.at[i, n],
            recv_sem=a_recv.at[i, n],
            device_id=(ahead, behind)[way][h],
            device_id_type=MESH,
        )

    def compute(i):
        for h in range(2):
            z = z_of(h, i, 0)
            zq[i, h, 0, 0] = encode(z[:Q], 1)
            zq[i, h, 1, 0] = encode(z[Q:], 1)
            message(i, h, 0, 0).start()
            message(i, h, 1, 0).start()
        for h in range(2):
            z = z_of(h, i, 1)
            zf[i, h, 0] = z[:Q]
            zq[i, h, 0, 1] = encode(z[Q:], 1)
            message(i, h, 0, 1).start()
            z = z_of(h, i, 2)
            zq[i, h, 1, 1] = encode(z[:Q], 1)
            zf[i, h, 1] = z[Q:]
            message(i, h, 1, 1).start()
        for h in range(2):
            z = z_of(h, i, 3)
            s1[i, h] = z

    def forward(i):
        for h in range(2):
            for way in range(2):
                message(i, h, way, 0).wait_recv()
                z2[i, h, way] = encode(zf[i, h, way] + decode(relay[i, h, way], 1), 2)
                message(i, h, way, 2).start()

    def message2(g, h, way, kind):
        n = (h * 2 + way) * 3 + kind
        source = s1m.at[g, h, way] if kind == 2 else s1q.at[g, h, way, kind]
        target = relay2.at[g, h, way] if kind == 0 else got2.at[g, h, way, kind - 1]
        return pltpu.make_async_remote_copy(
            src_ref=source,
            dst_ref=target,
            send_sem=b_send.at[g, n],
            recv_sem=b_recv.at[g, n],
            device_id=(ahead, behind)[way][1 - h],
            device_id_type=MESH,
        )

    def gather_in(i):
        g, j = i // 4, lax.rem(i, 4)
        for h in range(2):
            for way in range(2):
                message(i, h, way, 1).wait_recv()
                message(i, h, way, 2).wait_recv()
            s1[i, h, :Q] += decode(got[i, h, 0, 1], 2) + decode(got[i, h, 1, 0], 1)
            s1[i, h, Q:] += decode(got[i, h, 0, 0], 1) + decode(got[i, h, 1, 1], 2)

        @pl.when(j == 0)
        def _():
            for h in range(2):
                s1q[g, h, 0, 0] = encode(s1[i, h, :Q], 4)
                s1q[g, h, 1, 0] = encode(s1[i, h, Q:], 4)
                message2(g, h, 0, 0).start()
                message2(g, h, 1, 0).start()

        @pl.when(j == 1)
        def _():
            for h in range(2):
                s1q[g, h, 0, 1] = encode(s1[i, h, Q:], 4)
                message2(g, h, 0, 1).start()

        @pl.when(j == 2)
        def _():
            for h in range(2):
                s1q[g, h, 1, 1] = encode(s1[i, h, :Q], 4)
                message2(g, h, 1, 1).start()
            for h in range(2):
                for way in range(2):
                    message2(g, h, way, 0).wait_recv()
                    rows = slice(0, Q) if way == 0 else slice(Q, H)
                    s1m[g, h, way] = encode(
                        s1[i - 1 + way, h, rows] + decode(relay2[g, h, way], 4), 8
                    )
                    message2(g, h, way, 2).start()

    def cross_z():
        return pltpu.make_async_remote_copy(
            src_ref=s2q,
            dst_ref=gotz,
            send_sem=z_send,
            recv_sem=z_recv,
            device_id=across,
            device_id_type=MESH,
        )

    def finish(g):
        i = g * 4 + 3
        for h in range(2):
            for way in range(2):
                message2(g, h, way, 1).wait_recv()
                message2(g, h, way, 2).wait_recv()
            s2[h, :Q] = (
                s1[i, h, :Q] + decode(got2[g, h, 0, 1], 8) + decode(got2[g, h, 1, 0], 4)
            )
            s2[h, Q:] = (
                s1[i, h, Q:] + decode(got2[g, h, 0, 0], 4) + decode(got2[g, h, 1, 1], 8)
            )

    @pl.loop(0, SLOTS + 3)
    def _(i):
        @pl.when(i < SLOTS)
        def _():
            compute(i)

        @pl.when((i >= 1) & (i < SLOTS + 1))
        def _():
            forward(i - 1)

        @pl.when((i >= 2) & (i < SLOTS + 2))
        def _():
            gather_in(i - 2)

        @pl.when(i == 6)
        def _():
            finish(0)
            for h in range(2):
                s2q[h] = encode(s2[h], 16)
            cross_z().start()

    finish(1)
    cross_z().wait_recv()
    for h in range(2):
        out[h] = s2[h] + decode(gotz[h], 16)

    @pl.loop(0, SLOTS)
    def _(i):
        for h in range(2):
            for way in range(2):
                for kind in range(3):
                    message(i, h, way, kind).wait_send()

    @pl.loop(0, 2)
    def _(g):
        for h in range(2):
            for way in range(2):
                for kind in range(3):
                    message2(g, h, way, kind).wait_send()

    cross_z().wait_send()


def body(bold_series, seed_index):
    bf16, f32, i16 = jnp.bfloat16, jnp.float32, jnp.int16
    dma = pltpu.SemaphoreType.DMA
    summed = pl.pallas_call(
        kernel,
        out_shape=jax.ShapeDtypeStruct((2, H, TILE), f32),
        in_specs=[
            pl.BlockSpec(memory_space=pl.ANY),
            pl.BlockSpec(memory_space=pltpu.VMEM),
        ],
        out_specs=pl.BlockSpec(memory_space=pltpu.VMEM),
        scratch_shapes=[
            pltpu.VMEM((V // W, T, W), f32),
            pltpu.VMEM((TP, V), bf16),
            pltpu.VMEM((TP, K), f32),
            pltpu.VMEM((2, 4, PIECE, H), bf16),
            pltpu.VMEM((7, PIECE, H), bf16),
            pltpu.VMEM((PIECE, H), bf16),
            pltpu.VMEM((2, 4, PIECE, H), bf16),
            pltpu.VMEM((2, H, 384), bf16),
            pltpu.VMEM((SLOTS, 2, 2, Q, TILE), f32),
            pltpu.VMEM((SLOTS, 2, 2, 2, Q, TILE), i16),
            pltpu.VMEM((SLOTS, 2, 2, Q, TILE), i16),
            pltpu.VMEM((SLOTS, 2, 2, Q, TILE), i16),
            pltpu.VMEM((SLOTS, 2, 2, 2, Q, TILE), i16),
            pltpu.VMEM((SLOTS, 2, H, TILE), f32),
            pltpu.VMEM((2, 2, 2, 2, Q, TILE), i16),
            pltpu.VMEM((2, 2, 2, Q, TILE), i16),
            pltpu.VMEM((2, 2, 2, Q, TILE), i16),
            pltpu.VMEM((2, 2, 2, 2, Q, TILE), i16),
            pltpu.VMEM((2, H, TILE), f32),
            pltpu.VMEM((2, H, TILE), i16),
            pltpu.VMEM((2, H, TILE), i16),
            dma((V // W,)),
            dma((7,)), dma((7,)), dma((7,)), dma((7,)),
            dma((SLOTS, 12)), dma((SLOTS, 12)),
            dma((2, 12)), dma((2, 12)),
            dma, dma,
        ],
        compiler_params=pltpu.CompilerParams(
            collective_id=0, has_side_effects=True, vmem_limit_bytes=60 * 2**20
        ),
        name="group_z",
    )(bold_series.reshape(T, 1, V), seed_index.reshape(1, K))
    return summed.reshape(K, TILE).T * (1.0 / SUBJECTS)


def solution(mesh):
    split = Mesh(mesh.devices.reshape(4, 2, 4, 4, 2), AXES)
    return jax.shard_map(
        body,
        mesh=split,
        in_specs=(P(SUBJ, None, VOX), P()),
        out_specs=P(VOX + SUBJ, None),
        check_vma=False,
    )
```

time: 260 us -> 57 us (0.22)
  waiting for transfers between devices: 150 us -> 0 us
  Pallas kernels: 0 us -> 54.7 us
  blocking collectives: 36.5 us -> 0 us
  local copies, waits for them, and re-layouts: 32.2 us -> 0.84 us
  other arithmetic: 22 us -> 0.97 us
  between operations: 13.2 us -> 0.01 us
  matrix products: 5.17 us -> 0 us
    reduce_scatter x3 -> x0, waiting for transfers between devices: 150 us -> none  [sum_in_order(): parts = lax.psum_scatter(parts, axes[k], scatter_dimension=0, tiled=True)]
    pallas_call x0 -> x1, Pallas kernels: none -> 54.7 us  [body(): pl.pallas_call(kernel, out_shape=jax.ShapeDtypeStruct((2, H, TILE), f32),...]
    all_to_all x1 -> x0, blocking collectives: 36.5 us -> none  [from_everyone(): lax.all_to_all(jnp.broadcast_to(shard[None], (length, *shard.shape)), axi...]
    unnamed x5 -> x0, local copies, waits for them, and re-layouts: 23.4 us -> none
    reduce_sum x3 -> x0, other arithmetic: 16 us -> none  [the longest x1 8.82 us: normalize(): demean_series = series - jnp.mean(series, axis=0, keepdims=True)]
    dot_general x1 -> x0, matrix products: 5.17 us -> none  [correlate(): lax.dot_general(normed, seed_panel, (((0,), (0,)), ((), ())), preferred_e...]
    gather x1 -> x0, local copies, waits for them, and re-layouts: 4.74 us -> none  [body(): picked = jnp.take(normed, jnp.clip(offsets, 0, columns - 1), axis=1)]
    convert_element_type x2 -> x0, other arithmetic: 4.3 us -> none  [the longest x1 4.16 us: normalize(): return (demean_series * lax.rsqrt(spread + epsilon)).astype(jnp.bfloat16)]
  transfers between devices with their start and end apart: 3 -> 0, of which waited for: 3 -> 0; matrix products, arithmetic and copies ran while one was open for 0% -> 0% of each run, Pallas kernels for 0% -> 0%
where the time goes in v1:
time: 57 us; the launch traced here: 56.5 us
  Pallas kernels  54.7 us (96%)
  other arithmetic  0.97 us (2%)
  local copies, waits for them, and re-layouts  0.84 us (1%)
    pallas_call x1, Pallas kernels, body(): pl.pallas_call(kernel, out_shape=jax.ShapeDtypeStruct((2, H, TILE), f32),...  54.7 us

profile of v1, /device:TPU:2, one launch (start us, length us, event | category | flops | bytes accessed | tf_op | source)
XLA Modules:
  0.0 56.5 jit_solution(11916327994929454332)
XLA Ops:
  0.0 54.7 %group_z.1 = f32[2,128,256]{2,1,0:T(8,128)} custom-call(f32[300,1,8192]{2,1,0:T(1,128)} %bitcast.4, s32[1,256]{1,0:T(1,128)} %bitcast.6), custom_call_target="tpu_custom_call" | custom-call | tf_op jit(solution)/shard_map/group_z/pallas_call | solution.py:352
  54.7 1.0 %broadcast_multiply_fusion = f32[2,128,256]{2,1,0:T(8,128)S(1)} fusion(f32[2,128,256]{2,1,0:T(8,128)} %group_z.1), kind=kLoop, calls=%fused_computation | loop fusion | flops 65536 | bytes 524288 | tf_op jit(solution)/shard_map/mul | solution.py:393
  55.7 0.8 %copy.3 = f32[256,256]{0,1:T(8,128)} copy(f32[256,256]{1,0:T(8,128)S(1)} %bitcast.5) | data formatting | bytes 524288 | tf_op jit(solution)/shard_map/mul | solution.py:393

commit v2 on v0

v2 whole, which is shorter than its diff:
```python
import functools

import jax
import jax.numpy as jnp
from jax import lax
from jax.experimental import pallas as pl
from jax.experimental.pallas import tpu as pltpu
from jax.sharding import Mesh
from jax.sharding import PartitionSpec as P

AXES = ("x", "zh", "y", "zl", "c")
SUBJ = ("x", "zh", "y")
VOX = ("zl", "c")

CLIP = 0.99
EPS = 1e-05
LIMIT = 2.6466525

T = 300
TP = 304
PIECE = 80
V = 8192
K = 256
LENT = 2
TILE = 256
W = 1024
B = 512
H = K // 2
Q = K // 4
SUBJECTS = 32

MESH = pl.DeviceIdType.MESH


def step_of(terms):
    return 32700.0 / (terms * LIMIT) ** 0.5


def encode(z, terms):
    root = z * lax.rsqrt(jnp.maximum(jnp.abs(z), 1e-30))
    return jnp.round(root * step_of(terms)).astype(jnp.int32).astype(jnp.int16)


def code(c):
    return jnp.round(c * (32700.0 / CLIP)).astype(jnp.int32).astype(jnp.int16)


def plain(q):
    return q.astype(jnp.int32).astype(jnp.float32) * (CLIP / 32700.0)


def decode(q, terms):
    r = q.astype(jnp.int32).astype(jnp.float32)
    return r * jnp.abs(r) * (1.0 / step_of(terms) ** 2)


def clipped(cross):
    return jnp.clip(cross * (1.0 / T), -CLIP, CLIP)


def fisher(c):
    return 0.5 * (jnp.log(1.0 + c) - jnp.log(1.0 - c))


def kernel(
    bold, seeds, out,
    chosen_seeds, raw, normed, acc, panel, pieces, mine, full, theirs, seed_t, tiles,
    zf, m3, got, cq, gotd, s1, s1q, s1m, relay2, got2, s2, s2q, gotz,
    seed_sem, load_sem, rs_send, rs_recv, ag_send, ag_recv, p_send, p_recv, t_send, t_recv,
    a_send, a_recv, d_send, d_recv, b_send, b_recv, z_send, z_recv,
):
    x, zh, y, zl, c = (lax.axis_index(a) for a in AXES)
    side, place = zl // 2, lax.rem(zl, 2)

    def there(dz):
        return (3 - 3 * side, 2 - side, side * 2 + 1 - place, zl)[dz]

    peers = [(dz, dc) for dz in range(3) for dc in range(2)] + [(3, 1)]

    def group(dz, dc):
        return {"zl": there(dz), "c": lax.rem(c + dc, 2)}

    def step(g, way):
        return ({"x": lax.rem(x + 1 + 2 * way, 4)}, {"y": lax.rem(y + 1 + 2 * way, 4)})[g]

    across = {"zh": 1 - zh}

    barrier = pltpu.get_barrier_semaphore()
    everyone = [group(*p) for p in peers]
    everyone += [step(g, way) for g in range(2) for way in range(2)] + [across]
    for other in everyone:
        pl.semaphore_signal(barrier, inc=1, device_id=other, device_id_type=MESH)

    def turn(j):
        return lax.rem(2 - j + 3 * (j // 2) + 2 * (j // 3), 4)

    def plane(g):
        return lax.rem(zh + 1 + g, 2)

    def target(g, j, off):
        if g == 0:
            xt, yt = lax.rem(x + off, 4), lax.rem(y + turn(j), 4)
        else:
            xt, yt = lax.rem(x + turn(j), 4), lax.rem(y + off, 4)
        return (xt * 2 + plane(g)) * 4 + yt

    def line(p, g):
        return lax.rem(x + turn(p), 4) * 2 + plane(g)

    def load(p, g):
        first = pl.multiple_of(line(p, g) * W, W)
        return pltpu.make_async_copy(
            bold.at[:, 0, pl.ds(first, W)], raw.at[p, g], load_sem.at[p, g]
        )

    seed_copy = pltpu.make_async_copy(seeds, chosen_seeds, seed_sem)
    seed_copy.start()

    @pl.loop(0, 4)
    def _(p):
        for g in range(2):
            load(p, g).start()

    acc[...] = jnp.zeros_like(acc)

    def normalize(p, g):
        for j in range(W // B):
            series = raw[p, g, :, j * B : (j + 1) * B]
            center = series - jnp.sum(series, axis=0, keepdims=True) * (1.0 / T)
            spread = jnp.sum(center * center, axis=0, keepdims=True) * (1.0 / T)
            result = (center * lax.rsqrt(spread + EPS)).astype(jnp.bfloat16)
            for k in range(B // TILE):
                s = line(p, g) * 4 + j * (B // TILE) + k
                normed[s, T - T % 16 :] = jnp.zeros((TP - T + T % 16, TILE), jnp.bfloat16)
                normed[s, :T] = result[:, k * TILE : (k + 1) * TILE]

    def pick(p, g):
        ids = lax.broadcasted_iota(jnp.int32, (W, K), 0)
        wanted = chosen_seeds[...] - (zl * 2 + c) * V - line(p, g) * W
        chosen = jnp.where(ids == wanted, 1.0, 0.0).astype(jnp.bfloat16)
        total = acc[:TP]
        for k in range(W // TILE):
            total += jnp.dot(
                normed[line(p, g) * 4 + k],
                chosen[k * TILE : (k + 1) * TILE],
                preferred_element_type=jnp.float32,
            )
        acc[:TP] = total

    def leaf(i, kind, s, to):
        return pltpu.make_async_remote_copy(
            src_ref=normed.at[s],
            dst_ref=tiles.at[i, kind],
            send_sem=t_send.at[i, kind],
            recv_sem=t_recv.at[i, kind],
            device_id=to,
            device_id_type=MESH,
        )

    seed_copy.wait()

    @pl.loop(0, 4)
    def _(p):
        with jax.named_scope("loadwait"):
            load(p, 0).wait()
        normalize(p, 0)

        @pl.when(p == 0)
        def _():
            with jax.named_scope("barrier"):
                pl.semaphore_wait(barrier, len(everyone))
            for j in range(4):
                leaf(j, 0, target(0, j, 2), step(0, j % 2)).start()

        @pl.when(p == 1)
        def _():
            for j in range(1, LENT, 2):
                leaf(j, 1, target(0, j, 1), step(0, 0)).start()

        @pl.when(p == 2)
        def _():
            for j in range(0, LENT, 2):
                leaf(j, 1, target(0, j, 3), step(0, 1)).start()

        load(p, 1).wait()
        pick(p, 0)
        normalize(p, 1)
        way = lax.rem(p, 2)
        leaf(4 + p, 0, target(1, p, 2), step(1, way)).start()

        @pl.when(p < LENT)
        def _():
            leaf(4 + p, 1, target(1, p, 3 - 2 * way), step(1, 1 - way)).start()

        pick(p, 1)

    for h in range(2):
        for p in range(4):
            panel[h, p] = acc[p * PIECE : (p + 1) * PIECE, h * H : (h + 1) * H].astype(
                jnp.bfloat16
            )

    here = zl * 2 + c

    def scatter(n, source):
        to = group(*peers[n])
        return pltpu.make_async_remote_copy(
            src_ref=panel.at[to["c"], to["zl"]],
            dst_ref=pieces.at[source],
            send_sem=rs_send.at[n],
            recv_sem=rs_recv.at[source],
            device_id=to,
            device_id_type=MESH,
        )

    def share(n, source):
        return pltpu.make_async_remote_copy(
            src_ref=mine,
            dst_ref=full.at[lax.rem(source, 2), source // 2],
            send_sem=ag_send.at[n],
            recv_sem=ag_recv.at[source],
            device_id=group(*peers[n]),
            device_id_type=MESH,
        )

    for n in range(len(peers)):
        scatter(n, here).start()
    total = panel[c, zl].astype(jnp.float32)
    for n in range(len(peers)):
        source = lax.rem(here + 1 + n, 8)
        with jax.named_scope("rs_wait"):
            scatter(n, source).wait_recv()
        total += pieces[source].astype(jnp.float32)
    mine[...] = total.astype(jnp.bfloat16)
    full[c, zl] = mine[...]
    for n in range(len(peers)):
        share(n, here).start()

    def lend(g, way, source):
        spot = (lax.rem(source, 2), source // 2)
        return pltpu.make_async_remote_copy(
            src_ref=full.at[spot],
            dst_ref=theirs.at[g, way].at[spot],
            send_sem=p_send.at[g, way, source],
            recv_sem=p_recv.at[g, way, source],
            device_id=step(g, way),
            device_id_type=MESH,
        )

    def lend_all(source):
        for g in range(2):
            for way in range(2):
                lend(g, way, source).start()

    lend_all(here)
    for n, (dz, dc) in reversed(list(enumerate(peers))):
        source = there(dz) * 2 + lax.rem(c + dc, 2)
        with jax.named_scope("ag_wait"):
            share(n, source).wait_recv()
        lend_all(source)

    def turned(n, source):
        for h in range(2):
            whole = jnp.concatenate(
                [source[h, p].astype(jnp.float32) for p in range(4)]
                + [jnp.zeros((384 - 4 * PIECE, H), jnp.float32)],
                axis=0,
            )
            seed_t[n, h] = whole.T.astype(jnp.bfloat16)

    turned(0, full)

    def c_of(n, h, series):
        cross = jnp.dot(seed_t[n, h][:, :TP], series, preferred_element_type=jnp.float32)
        return clipped(cross)

    def z_of(n, h, series):
        return fisher(c_of(n, h, series))

    slots = [(g, w) for g in range(2) for w in range(2)]

    def direct(g, j, h):
        return pltpu.make_async_remote_copy(
            src_ref=cq.at[g * 4 + j, h],
            dst_ref=gotd.at[g * 4 + j, h],
            send_sem=d_send.at[g * 4 + j, h],
            recv_sem=d_recv.at[g * 4 + j, h],
            device_id=step(g, 1 - j % 2),
            device_id_type=MESH,
        )

    for g in range(2):
        for h in range(2):
            for j in range(LENT, 4):
                series = normed[target(g, j, 3 - 2 * (j % 2))]
                cq[g * 4 + j, h] = code(c_of(0, h, series))
            for j in range(LENT, 4):
                direct(g, j, h).start()

    with jax.named_scope("own"):

        @pl.loop(0, 2)
        def _(jj):
            for g, w in slots:
                j = 2 * jj + w
                for h in range(2):
                    zf[g * 4 + j, h] = z_of(0, h, normed[target(g, j, 1 + 2 * w)])
                    s1[g * 4 + j, h] = z_of(0, h, normed[target(g, j, 0)])

    def borrow(g):
        for way in range(2):
            with jax.named_scope("lendwait"):
                for source in range(8):
                    lend(g, way, source).wait_recv()
            turned(1 + 2 * g + way, theirs.at[g, way])

    def summed(g, j, h):
        return pltpu.make_async_remote_copy(
            src_ref=m3.at[g * 4 + j, h],
            dst_ref=got.at[g * 4 + j, h],
            send_sem=a_send.at[g * 4 + j, h],
            recv_sem=a_recv.at[g * 4 + j, h],
            device_id=step(g, j % 2),
            device_id_type=MESH,
        )

    def came(g, j, kind):
        return leaf(g * 4 + j, kind, 0, step(g, 0))

    def far(g, h):
        if h == 0:
            for j in range(4):
                came(g, j, 0).wait_recv()
        for j in range(4):
            i, w = g * 4 + j, j % 2
            m3[i, h] = encode(zf[i, h] + z_of(1 + 2 * g + w, h, tiles[i, 0]), 2)
        for j in range(4):
            summed(g, j, h).start()

    def near(g, h):
        for j in range(4):
            if h == 0 and j < LENT:
                came(g, j, 1).wait_recv()
            if j >= LENT:
                direct(g, j, h).wait_recv()
        for j in range(4):
            i, w = g * 4 + j, j % 2
            if j < LENT:
                s1[i, h] += z_of(2 + 2 * g - w, h, tiles[i, 1])
            else:
                s1[i, h] += fisher(plain(gotd[g * 4 + j, h]))

    rows = (slice(0, Q), slice(Q, H))

    def message2(g, h, way, kind):
        return pltpu.make_async_remote_copy(
            src_ref=s1m.at[g, h, way] if kind == 2 else s1q.at[g, h, way, kind],
            dst_ref=relay2.at[g, h, way] if kind == 0 else got2.at[g, h, way, kind - 1],
            send_sem=b_send.at[g, h, way, kind],
            recv_sem=b_recv.at[g, h, way, kind],
            device_id=step(1 - g, way),
            device_id_type=MESH,
        )

    def add_in(g, h, j):
        with jax.named_scope("m3wait"):
            summed(g, j, h).wait_recv()
        s1[g * 4 + j, h] += decode(got[g * 4 + j, h], 2)

    def cross_z(h):
        return pltpu.make_async_remote_copy(
            src_ref=s2q.at[h],
            dst_ref=gotz.at[h],
            send_sem=z_send.at[h],
            recv_sem=z_recv.at[h],
            device_id=across,
            device_id_type=MESH,
        )

    def second(g, h):
        add_in(g, h, 0)
        for way in range(2):
            s1q[g, h, way, 0] = encode(s1[g * 4, h, rows[way]], 4)
            message2(g, h, way, 0).start()
        add_in(g, h, 1)
        s1q[g, h, 0, 1] = encode(s1[g * 4 + 1, h, rows[1]], 4)
        message2(g, h, 0, 1).start()

    def third(g, h):
        add_in(g, h, 2)
        s1q[g, h, 1, 1] = encode(s1[g * 4 + 2, h, rows[0]], 4)
        message2(g, h, 1, 1).start()
        for way in range(2):
            with jax.named_scope("relaywait"):
                message2(g, h, way, 0).wait_recv()
            s1m[g, h, way] = encode(
                s1[g * 4 + 1 + way, h, rows[way]] + decode(relay2[g, h, way], 4), 8
            )
            message2(g, h, way, 2).start()
        add_in(g, h, 3)

    def finish(g, h):
        for way in range(2):
            with jax.named_scope("finwait"):
                message2(g, h, 1 - way, 1).wait_recv()
                message2(g, h, way, 2).wait_recv()
            s2[g, h, rows[way]] = (
                s1[g * 4 + 3, h, rows[way]]
                + decode(got2[g, h, 1 - way, 0], 4)
                + decode(got2[g, h, way, 1], 8)
            )
        if g == 0:
            s2q[h] = encode(s2[g, h], 16)
            cross_z(h).start()

    borrow(0)
    with jax.named_scope("far0"):
        far(0, 0)
        far(0, 1)
    borrow(1)
    far(1, 0)
    with jax.named_scope("near0"):
        near(0, 0)
        near(0, 1)
    second(0, 0)
    near(1, 0)
    second(0, 1)
    far(1, 1)
    third(0, 0)
    near(1, 1)
    second(1, 0)
    third(0, 1)
    finish(0, 0)
    second(1, 1)
    finish(0, 1)
    third(1, 0)
    third(1, 1)
    for h in range(2):
        finish(1, h)
        with jax.named_scope("zwait"):
            cross_z(h).wait_recv()
        out[:, h * H : (h + 1) * H] = (
            (s2[1, h] + decode(gotz[h], 16)) * (1.0 / SUBJECTS)
        ).T

    for n in range(len(peers)):
        scatter(n, here).wait_send()
        share(n, here).wait_send()
    for g in range(2):
        for way in range(2):
            for source in range(8):
                lend(g, way, source).wait_send()
            for h in range(2):
                for kind in range(3):
                    message2(g, h, way, kind).wait_send()
        for j in range(4):
            came(g, j, 0).wait_send()
            if j < LENT:
                came(g, j, 1).wait_send()
            for h in range(2):
                summed(g, j, h).wait_send()
                if j >= LENT:
                    direct(g, j, h).wait_send()
    for h in range(2):
        cross_z(h).wait_send()


def body(bold_series, seed_index):
    bf16, f32, i16 = jnp.bfloat16, jnp.float32, jnp.int16
    dma = pltpu.SemaphoreType.DMA
    return pl.pallas_call(
        kernel,
        out_shape=jax.ShapeDtypeStruct((TILE, K), f32),
        in_specs=[
            pl.BlockSpec(memory_space=pltpu.HBM),
            pl.BlockSpec(memory_space=pltpu.HBM),
        ],
        out_specs=pl.BlockSpec(memory_space=pltpu.VMEM),
        scratch_shapes=[
            pltpu.VMEM((1, K), jnp.int32),
            pltpu.VMEM((4, 2, T, W), f32),
            pltpu.VMEM((V // TILE, TP, TILE), bf16),
            pltpu.VMEM((4 * PIECE, K), f32),
            pltpu.VMEM((2, 4, PIECE, H), bf16),
            pltpu.VMEM((8, PIECE, H), bf16),
            pltpu.VMEM((PIECE, H), bf16),
            pltpu.VMEM((2, 4, PIECE, H), bf16),
            pltpu.VMEM((2, 2, 2, 4, PIECE, H), bf16),
            pltpu.VMEM((5, 2, H, 384), bf16),
            pltpu.VMEM((8, 2, TP, TILE), bf16),
            pltpu.VMEM((8, 2, H, TILE), f32),
            pltpu.VMEM((8, 2, H, TILE), i16),
            pltpu.VMEM((8, 2, H, TILE), i16),
            pltpu.VMEM((8, 2, H, TILE), i16),
            pltpu.VMEM((8, 2, H, TILE), i16),
            pltpu.VMEM((8, 2, H, TILE), f32),
            pltpu.VMEM((2, 2, 2, 2, Q, TILE), i16),
            pltpu.VMEM((2, 2, 2, Q, TILE), i16),
            pltpu.VMEM((2, 2, 2, Q, TILE), i16),
            pltpu.VMEM((2, 2, 2, 2, Q, TILE), i16),
            pltpu.VMEM((2, 2, H, TILE), f32),
            pltpu.VMEM((2, H, TILE), i16),
            pltpu.VMEM((2, H, TILE), i16),
            dma,
            dma((4, 2)),
            dma((7,)), dma((8,)), dma((7,)), dma((8,)),
            dma((2, 2, 8)), dma((2, 2, 8)), dma((8, 2)), dma((8, 2)),
            dma((8, 2)), dma((8, 2)), dma((8, 2)), dma((8, 2)),
            dma((2, 2, 2, 3)), dma((2, 2, 2, 3)),
            dma((2,)), dma((2,)),
        ],
        compiler_params=pltpu.CompilerParams(
            collective_id=0, has_side_effects=True, vmem_limit_bytes=50 * 2**20
        ),
        name="group_z",
    )(bold_series.reshape(T, 1, V), seed_index.reshape(1, K))


def solution(mesh):
    split = Mesh(mesh.devices.reshape(4, 2, 4, 4, 2), AXES)
    return jax.shard_map(
        body,
        mesh=split,
        in_specs=(P(SUBJ, None, VOX), P()),
        out_specs=P(VOX + SUBJ, None),
        check_vma=False,
    )
```

time: 260 us -> 53.8 us (0.21)
  waiting for transfers between devices: 150 us -> 0 us
  Pallas kernels: 0 us -> 52.4 us
  blocking collectives: 36.5 us -> 0 us
  local copies, waits for them, and re-layouts: 32.2 us -> 1.38 us
  other arithmetic: 22 us -> 0 us
  between operations: 13.2 us -> 0.01 us
  matrix products: 5.17 us -> 0 us
    reduce_scatter x3 -> x0, waiting for transfers between devices: 150 us -> none  [sum_in_order(): parts = lax.psum_scatter(parts, axes[k], scatter_dimension=0, tiled=True)]
    pallas_call x0 -> x1, Pallas kernels: none -> 52.4 us  [body(): pl.pallas_call(kernel, out_shape=jax.ShapeDtypeStruct((TILE, K), f32), in...]
    all_to_all x1 -> x0, blocking collectives: 36.5 us -> none  [from_everyone(): lax.all_to_all(jnp.broadcast_to(shard[None], (length, *shard.shape)), axi...]
    unnamed x5 -> x3, local copies, waits for them, and re-layouts: 23.4 us -> 1.38 us
    reduce_sum x3 -> x0, other arithmetic: 16 us -> none  [the longest x1 8.82 us: normalize(): demean_series = series - jnp.mean(series, axis=0, keepdims=True)]
    dot_general x1 -> x0, matrix products: 5.17 us -> none  [correlate(): lax.dot_general(normed, seed_panel, (((0,), (0,)), ((), ())), preferred_e...]
    gather x1 -> x0, local copies, waits for them, and re-layouts: 4.74 us -> none  [body(): picked = jnp.take(normed, jnp.clip(offsets, 0, columns - 1), axis=1)]
    convert_element_type x2 -> x0, other arithmetic: 4.3 us -> none  [the longest x1 4.16 us: normalize(): return (demean_series * lax.rsqrt(spread + epsilon)).astype(jnp.bfloat16)]
  transfers between devices with their start and end apart: 3 -> 0, of which waited for: 3 -> 0; matrix products, arithmetic and copies ran while one was open for 0% -> 0% of each run, Pallas kernels for 0% -> 0%
where the time goes in v2:
time: 53.8 us
  Pallas kernels  52.4 us (97%)
  local copies, waits for them, and re-layouts  1.38 us (3%)
    pallas_call x1, Pallas kernels, body(): pl.pallas_call(kernel, out_shape=jax.ShapeDtypeStruct((TILE, K), f32), in...  52.4 us
    unnamed x3, local copies, waits for them, and re-layouts  1.38 us

profile of v2, /device:TPU:2, one launch (start us, length us, event | category | flops | bytes accessed | tf_op | source)
XLA Modules:
  0.0 53.8 jit_solution(15072212130322253574)
XLA Ops:
  0.0 0.0 copy-start
  0.0 0.7 %copy-done = s32[256]{0:T(256)S(1)} copy-done((s32[256]{0:T(256)S(1)}, s32[256]{0:T(256)}, u32[]{:S(2)}) %copy-start) | copy-done | bytes 1048
  0.7 52.4 %group_z.1 = f32[256,256]{1,0:T(8,128)S(1)} custom-call(f32[300,1,8192]{2,1,0:T(1,128)} %bitcast.3, s32[1,256]{1,0:T(1,128)S(1)} %bitcast.2), custom_call_target="tpu_custom_call" | custom-call | tf_op jit(solution)/shard_map/group_z/pallas_call | solution.py:471
  53.1 0.7 %copy.4 = f32[256,256]{1,0:T(8,128)} copy(f32[256,256]{1,0:T(8,128)S(1)} %group_z.1) | data formatting | bytes 524288
Async XLA Ops:
  0.0 0.7 %copy-start = (s32[256]{0:T(256)S(1)}, s32[256]{0:T(256)}, u32[]{:S(2)}) copy-start(s32[256]{0:T(256)} %param.3) | copy-start | bytes 3076

commit v3 on v2

--- a/solution.py
+++ b/solution.py
@@ -21,7 +21,7 @@
 PIECE = 80
 V = 8192
 K = 256
-LENT = 2
+LENT = 3
 TILE = 256
 W = 1024
 B = 512
@@ -64,9 +64,9 @@
 
 def kernel(
     bold, seeds, out,
-    chosen_seeds, raw, normed, acc, panel, pieces, mine, full, theirs, seed_t, tiles,
+    chosen_seeds, raw, normed, acc, panel, half, both, pieces, full, theirs, seed_t, tiles,
     zf, m3, got, cq, gotd, s1, s1q, s1m, relay2, got2, s2, s2q, gotz,
-    seed_sem, load_sem, rs_send, rs_recv, ag_send, ag_recv, p_send, p_recv, t_send, t_recv,
+    seed_sem, load_sem, h_send, h_recv, rs_send, rs_recv, ag_send, ag_recv, c_send, p_send, p_recv, t_send, t_recv,
     a_send, a_recv, d_send, d_recv, b_send, b_recv, z_send, z_recv,
 ):
     x, zh, y, zl, c = (lax.axis_index(a) for a in AXES)
@@ -75,23 +75,20 @@
     def there(dz):
         return (3 - 3 * side, 2 - side, side * 2 + 1 - place, zl)[dz]
 
-    peers = [(dz, dc) for dz in range(3) for dc in range(2)] + [(3, 1)]
-
-    def group(dz, dc):
-        return {"zl": there(dz), "c": lax.rem(c + dc, 2)}
-
     def step(g, way):
         return ({"x": lax.rem(x + 1 + 2 * way, 4)}, {"y": lax.rem(y + 1 + 2 * way, 4)})[g]
 
     across = {"zh": 1 - zh}
 
     barrier = pltpu.get_barrier_semaphore()
-    everyone = [group(*p) for p in peers]
+    everyone = [{"zl": there(dz)} for dz in range(3)] + [{"c": 1 - c}]
     everyone += [step(g, way) for g in range(2) for way in range(2)] + [across]
     for other in everyone:
         pl.semaphore_signal(barrier, inc=1, device_id=other, device_id_type=MESH)
 
     def turn(j):
+        if isinstance(j, int):
+            return (2, 1, 3, 0)[j]
         return lax.rem(2 - j + 3 * (j // 2) + 2 * (j // 3), 4)
 
     def plane(g):
@@ -159,40 +156,30 @@
 
     seed_copy.wait()
 
-    @pl.loop(0, 4)
-    def _(p):
+    def give(p, g):
+        if g == 1:
+            leaf(4 + p, 0, target(1, p, 2), step(1, p % 2)).start()
+            if p < LENT:
+                leaf(4 + p, 1, target(1, p, 3 - 2 * (p % 2)), step(1, 1 - p % 2)).start()
+        elif p == 0:
+            for j in range(4):
+                leaf(j, 0, target(0, j, 2), step(0, j % 2)).start()
+        elif p < 3:
+            for j in range(2 - p, LENT, 2):
+                leaf(j, 1, target(0, j, 2 * p - 1), step(0, p - 1)).start()
+
+    order = [(p, g) for p in range(4) for g in range(2)]
+    for n, (p, g) in enumerate(order):
         with jax.named_scope("loadwait"):
-            load(p, 0).wait()
-        normalize(p, 0)
-
-        @pl.when(p == 0)
-        def _():
+            load(p, g).wait()
+        if n:
+            pick(*order[n - 1])
+        normalize(p, g)
+        if n == 0:
             with jax.named_scope("barrier"):
                 pl.semaphore_wait(barrier, len(everyone))
-            for j in range(4):
-                leaf(j, 0, target(0, j, 2), step(0, j % 2)).start()
-
-        @pl.when(p == 1)
-        def _():
-            for j in range(1, LENT, 2):
-                leaf(j, 1, target(0, j, 1), step(0, 0)).start()
-
-        @pl.when(p == 2)
-        def _():
-            for j in range(0, LENT, 2):
-                leaf(j, 1, target(0, j, 3), step(0, 1)).start()
-
-        load(p, 1).wait()
-        pick(p, 0)
-        normalize(p, 1)
-        way = lax.rem(p, 2)
-        leaf(4 + p, 0, target(1, p, 2), step(1, way)).start()
-
-        @pl.when(p < LENT)
-        def _():
-            leaf(4 + p, 1, target(1, p, 3 - 2 * way), step(1, 1 - way)).start()
-
-        pick(p, 1)
+        give(p, g)
+    pick(*order[-1])
 
     for h in range(2):
         for p in range(4):
@@ -202,39 +189,65 @@
 
     here = zl * 2 + c
 
-    def scatter(n, source):
-        to = group(*peers[n])
-        return pltpu.make_async_remote_copy(
-            src_ref=panel.at[to["c"], to["zl"]],
+    partner = {"c": 1 - c}
+
+    def halve():
+        return pltpu.make_async_remote_copy(
+            src_ref=panel.at[1 - c],
+            dst_ref=half,
+            send_sem=h_send,
+            recv_sem=h_recv,
+            device_id=partner,
+            device_id_type=MESH,
+        )
+
+    def scatter(dz, source):
+        return pltpu.make_async_remote_copy(
+            src_ref=both.at[there(dz)],
             dst_ref=pieces.at[source],
-            send_sem=rs_send.at[n],
+            send_sem=rs_send.at[dz],
             recv_sem=rs_recv.at[source],
-            device_id=to,
-            device_id_type=MESH,
-        )
-
-    def share(n, source):
-        return pltpu.make_async_remote_copy(
-            src_ref=mine,
-            dst_ref=full.at[lax.rem(source, 2), source // 2],
-            send_sem=ag_send.at[n],
-            recv_sem=ag_recv.at[source],
-            device_id=group(*peers[n]),
-            device_id_type=MESH,
-        )
-
-    for n in range(len(peers)):
-        scatter(n, here).start()
-    total = panel[c, zl].astype(jnp.float32)
-    for n in range(len(peers)):
-        source = lax.rem(here + 1 + n, 8)
+            device_id={"zl": there(dz)},
+            device_id_type=MESH,
+        )
+
+    def share(dz, source):
+        return pltpu.make_async_remote_copy(
+            src_ref=full.at[c, zl],
+            dst_ref=full.at[c, source],
+            send_sem=ag_send.at[dz],
+            recv_sem=ag_recv.at[source * 2 + c],
+            device_id={"zl": there(dz)},
+            device_id_type=MESH,
+        )
+
+    def copy_over(core, source):
+        return pltpu.make_async_remote_copy(
+            src_ref=full.at[core, source],
+            dst_ref=full.at[core, source],
+            send_sem=c_send.at[source],
+            recv_sem=ag_recv.at[source * 2 + core],
+            device_id=partner,
+            device_id_type=MESH,
+        )
+
+    halve().start()
+    halve().wait_recv()
+    for p in range(4):
+        both[p] = (panel[c, p].astype(jnp.float32) + half[p].astype(jnp.float32)).astype(
+            jnp.bfloat16
+        )
+    for dz in range(3):
+        scatter(dz, zl).start()
+    total = both[zl].astype(jnp.float32)
+    for dz in (2, 1, 0):
         with jax.named_scope("rs_wait"):
-            scatter(n, source).wait_recv()
-        total += pieces[source].astype(jnp.float32)
-    mine[...] = total.astype(jnp.bfloat16)
-    full[c, zl] = mine[...]
-    for n in range(len(peers)):
-        share(n, here).start()
+            scatter(dz, there(dz)).wait_recv()
+        total += pieces[there(dz)].astype(jnp.float32)
+    full[c, zl] = total.astype(jnp.bfloat16)
+    for dz in range(3):
+        share(dz, zl).start()
+    copy_over(c, zl).start()
 
     def lend(g, way, source):
         spot = (lax.rem(source, 2), source // 2)
@@ -253,11 +266,16 @@
                 lend(g, way, source).start()
 
     lend_all(here)
-    for n, (dz, dc) in reversed(list(enumerate(peers))):
-        source = there(dz) * 2 + lax.rem(c + dc, 2)
+    for dz, core in ((3, 1), (2, 0), (2, 1), (1, 0), (0, 0), (1, 1), (0, 1)):
+        source = there(dz)
         with jax.named_scope("ag_wait"):
-            share(n, source).wait_recv()
-        lend_all(source)
+            if core:
+                copy_over(1 - c, source).wait_recv()
+                lend_all(source * 2 + 1 - c)
+            else:
+                share(dz, source).wait_recv()
+                copy_over(c, source).start()
+                lend_all(source * 2 + c)
 
     def turned(n, source):
         for h in range(2):
@@ -294,6 +312,7 @@
             for j in range(LENT, 4):
                 series = normed[target(g, j, 3 - 2 * (j % 2))]
                 cq[g * 4 + j, h] = code(c_of(0, h, series))
+        for h in range(2):
             for j in range(LENT, 4):
                 direct(g, j, h).start()
 
@@ -305,7 +324,6 @@
                 j = 2 * jj + w
                 for h in range(2):
                     zf[g * 4 + j, h] = z_of(0, h, normed[target(g, j, 1 + 2 * w)])
-                    s1[g * 4 + j, h] = z_of(0, h, normed[target(g, j, 0)])
 
     def borrow(g):
         for way in range(2):
@@ -346,9 +364,10 @@
         for j in range(4):
             i, w = g * 4 + j, j % 2
             if j < LENT:
-                s1[i, h] += z_of(2 + 2 * g - w, h, tiles[i, 1])
+                term = z_of(2 + 2 * g - w, h, tiles[i, 1])
             else:
-                s1[i, h] += fisher(plain(gotd[g * 4 + j, h]))
+                term = fisher(plain(gotd[i, h]))
+            s1[i, h] = z_of(0, h, normed[target(g, j, 0)]) + term
 
     rows = (slice(0, Q), slice(Q, H))
 
@@ -425,8 +444,8 @@
     second(0, 0)
     near(1, 0)
     second(0, 1)
+    third(0, 0)
     far(1, 1)
-    third(0, 0)
     near(1, 1)
     second(1, 0)
     third(0, 1)
@@ -443,9 +462,12 @@
             (s2[1, h] + decode(gotz[h], 16)) * (1.0 / SUBJECTS)
         ).T
 
-    for n in range(len(peers)):
-        scatter(n, here).wait_send()
-        share(n, here).wait_send()
+    halve().wait_send()
+    for dz in range(3):
+        scatter(dz, zl).wait_send()
+        share(dz, zl).wait_send()
+    for source in range(4):
+        copy_over(c, source).wait_send()
     for g in range(2):
         for way in range(2):
             for source in range(8):
@@ -482,8 +504,9 @@
             pltpu.VMEM((V // TILE, TP, TILE), bf16),
             pltpu.VMEM((4 * PIECE, K), f32),
             pltpu.VMEM((2, 4, PIECE, H), bf16),
-            pltpu.VMEM((8, PIECE, H), bf16),
-            pltpu.VMEM((PIECE, H), bf16),
+            pltpu.VMEM((4, PIECE, H), bf16),
+            pltpu.VMEM((4, PIECE, H), bf16),
+            pltpu.VMEM((4, PIECE, H), bf16),
             pltpu.VMEM((2, 4, PIECE, H), bf16),
             pltpu.VMEM((2, 2, 2, 4, PIECE, H), bf16),
             pltpu.VMEM((5, 2, H, 384), bf16),
@@ -503,7 +526,8 @@
             pltpu.VMEM((2, H, TILE), i16),
             dma,
             dma((4, 2)),
-            dma((7,)), dma((8,)), dma((7,)), dma((8,)),
+            dma, dma,
+            dma((3,)), dma((4,)), dma((3,)), dma((8,)), dma((4,)),
             dma((2, 2, 8)), dma((2, 2, 8)), dma((8, 2)), dma((8, 2)),
             dma((8, 2)), dma((8, 2)), dma((8, 2)), dma((8, 2)),
             dma((2, 2, 2, 3)), dma((2, 2, 2, 3)),

time: 53.8 us -> 51.1 us (0.950)
  Pallas kernels: 52.4 us -> 49.6 us
    pallas_call x1, Pallas kernels: 52.4 us -> 49.6 us  [body(): pl.pallas_call(kernel, out_shape=jax.ShapeDtypeStruct((TILE, K), f32), in...]
where the time goes in v3:
time: 51.1 us; the launch traced here: 51 us
  Pallas kernels  49.6 us (97%)
  local copies, waits for them, and re-layouts  1.38 us (3%)
    pallas_call x1, Pallas kernels, body(): pl.pallas_call(kernel, out_shape=jax.ShapeDtypeStruct((TILE, K), f32), in...  49.6 us
    unnamed x3, local copies, waits for them, and re-layouts  1.38 us

profile of v3, /device:TPU:2, one launch (start us, length us, event | category | flops | bytes accessed | tf_op | source)
XLA Modules:
  0.0 51.0 jit_solution(15946965846675245949)
XLA Ops:
  0.0 0.0 copy-start
  0.0 0.7 %copy-done = s32[256]{0:T(256)S(1)} copy-done((s32[256]{0:T(256)S(1)}, s32[256]{0:T(256)}, u32[]{:S(2)}) %copy-start) | copy-done | bytes 1048
  0.7 49.6 %group_z.1 = f32[256,256]{1,0:T(8,128)S(1)} custom-call(f32[300,1,8192]{2,1,0:T(1,128)} %bitcast.3, s32[1,256]{1,0:T(1,128)S(1)} %bitcast.2), custom_call_target="tpu_custom_call" | custom-call | tf_op jit(solution)/shard_map/group_z/pallas_call | solution.py:493
  50.3 0.7 %copy.4 = f32[256,256]{1,0:T(8,128)} copy(f32[256,256]{1,0:T(8,128)S(1)} %group_z.1) | data formatting | bytes 524288
Async XLA Ops:
  0.0 0.7 %copy-start = (s32[256]{0:T(256)S(1)}, s32[256]{0:T(256)}, u32[]{:S(2)}) copy-start(s32[256]{0:T(256)} %param.3) | copy-start | bytes 3076

commit v4 on v3

--- a/solution.py
+++ b/solution.py
@@ -386,12 +386,12 @@
             summed(g, j, h).wait_recv()
         s1[g * 4 + j, h] += decode(got[g * 4 + j, h], 2)
 
-    def cross_z(h):
-        return pltpu.make_async_remote_copy(
-            src_ref=s2q.at[h],
-            dst_ref=gotz.at[h],
-            send_sem=z_send.at[h],
-            recv_sem=z_recv.at[h],
+    def cross_z(h, way):
+        return pltpu.make_async_remote_copy(
+            src_ref=s2q.at[h, way],
+            dst_ref=gotz.at[h, way],
+            send_sem=z_send.at[h, way],
+            recv_sem=z_recv.at[h, way],
             device_id=across,
             device_id_type=MESH,
         )
@@ -428,9 +428,9 @@
                 + decode(got2[g, h, 1 - way, 0], 4)
                 + decode(got2[g, h, way, 1], 8)
             )
-        if g == 0:
-            s2q[h] = encode(s2[g, h], 16)
-            cross_z(h).start()
+            if g == 0:
+                s2q[h, way] = encode(s2[g, h, rows[way]], 16)
+                cross_z(h, way).start()
 
     borrow(0)
     with jax.named_scope("far0"):
@@ -457,10 +457,12 @@
     for h in range(2):
         finish(1, h)
         with jax.named_scope("zwait"):
-            cross_z(h).wait_recv()
-        out[:, h * H : (h + 1) * H] = (
-            (s2[1, h] + decode(gotz[h], 16)) * (1.0 / SUBJECTS)
-        ).T
+            for way in range(2):
+                cross_z(h, way).wait_recv()
+                s2[1, h, rows[way]] = (
+                    s2[1, h, rows[way]] + decode(gotz[h, way], 16)
+                ) * (1.0 / SUBJECTS)
+        out[:, h * H : (h + 1) * H] = s2[1, h].T
 
     halve().wait_send()
     for dz in range(3):
@@ -484,7 +486,8 @@
                 if j >= LENT:
                     direct(g, j, h).wait_send()
     for h in range(2):
-        cross_z(h).wait_send()
+        for way in range(2):
+            cross_z(h, way).wait_send()
 
 
 def body(bold_series, seed_index):
@@ -522,8 +525,8 @@
             pltpu.VMEM((2, 2, 2, Q, TILE), i16),
             pltpu.VMEM((2, 2, 2, 2, Q, TILE), i16),
             pltpu.VMEM((2, 2, H, TILE), f32),
-            pltpu.VMEM((2, H, TILE), i16),
-            pltpu.VMEM((2, H, TILE), i16),
+            pltpu.VMEM((2, 2, Q, TILE), i16),
+            pltpu.VMEM((2, 2, Q, TILE), i16),
             dma,
             dma((4, 2)),
             dma, dma,
@@ -531,13 +534,13 @@
             dma((2, 2, 8)), dma((2, 2, 8)), dma((8, 2)), dma((8, 2)),
             dma((8, 2)), dma((8, 2)), dma((8, 2)), dma((8, 2)),
             dma((2, 2, 2, 3)), dma((2, 2, 2, 3)),
-            dma((2,)), dma((2,)),
+            dma((2, 2)), dma((2, 2)),
         ],
         compiler_params=pltpu.CompilerParams(
             collective_id=0, has_side_effects=True, vmem_limit_bytes=50 * 2**20
         ),
         name="group_z",
-    )(bold_series.reshape(T, 1, V), seed_index.reshape(1, K))
+    )(bold_series.reshape(T, 1, V), pltpu.with_memory_space_constraint(seed_index.reshape(1, K), pltpu.HBM))
 
 
 def solution(mesh):

time: 51.1 us -> 50.5 us (0.988)
  local copies, waits for them, and re-layouts: 1.38 us -> 0.71 us
    unnamed x3 -> x1, local copies, waits for them, and re-layouts: 1.38 us -> 0.71 us
where the time goes in v4:
time: 50.5 us; the launch traced here: 50.4 us
  Pallas kernels  49.7 us (98%)
  local copies, waits for them, and re-layouts  0.71 us (1%)
    pallas_call x1, Pallas kernels, body(): pl.pallas_call(kernel, out_shape=jax.ShapeDtypeStruct((TILE, K), f32), in...  49.7 us

profile of v4, /device:TPU:2, one launch (start us, length us, event | category | flops | bytes accessed | tf_op | source)
XLA Modules:
  0.0 50.4 jit_solution(1077901180074293861)
XLA Ops:
  0.0 49.7 %group_z.1 = f32[256,256]{1,0:T(8,128)S(1)} custom-call(f32[300,1,8192]{2,1,0:T(1,128)} %bitcast.2, s32[1,256]{1,0:T(1,128)} %bitcast.3), custom_call_target="tpu_custom_call" | custom-call | tf_op jit(solution)/shard_map/group_z/pallas_call | solution.py:496
  49.7 0.7 %copy.4 = f32[256,256]{1,0:T(8,128)} copy(f32[256,256]{1,0:T(8,128)S(1)} %group_z.1) | data formatting | bytes 524288

commit v5 on v4

--- a/solution.py
+++ b/solution.py
@@ -104,10 +104,12 @@
     def line(p, g):
         return lax.rem(x + turn(p), 4) * 2 + plane(g)
 
-    def load(p, g):
-        first = pl.multiple_of(line(p, g) * W, W)
+    def load(p, g, j):
+        first = pl.multiple_of(line(p, g) * W + j * B, B)
         return pltpu.make_async_copy(
-            bold.at[:, 0, pl.ds(first, W)], raw.at[p, g], load_sem.at[p, g]
+            bold.at[:, 0, pl.ds(first, B)],
+            raw.at[p, g, :, pl.ds(j * B, B)],
+            load_sem.at[p, g, j],
         )
 
     seed_copy = pltpu.make_async_copy(seeds, chosen_seeds, seed_sem)
@@ -116,12 +118,15 @@
     @pl.loop(0, 4)
     def _(p):
         for g in range(2):
-            load(p, g).start()
+            for j in range(W // B):
+                load(p, g, j).start()
 
     acc[...] = jnp.zeros_like(acc)
 
     def normalize(p, g):
         for j in range(W // B):
+            if (p, g) == (0, 0):
+                load(p, g, j).wait()
             series = raw[p, g, :, j * B : (j + 1) * B]
             center = series - jnp.sum(series, axis=0, keepdims=True) * (1.0 / T)
             spread = jnp.sum(center * center, axis=0, keepdims=True) * (1.0 / T)
@@ -170,8 +175,9 @@
 
     order = [(p, g) for p in range(4) for g in range(2)]
     for n, (p, g) in enumerate(order):
-        with jax.named_scope("loadwait"):
-            load(p, g).wait()
+        if n:
+            for j in range(W // B):
+                load(p, g, j).wait()
         if n:
             pick(*order[n - 1])
         normalize(p, g)
@@ -528,7 +534,7 @@
             pltpu.VMEM((2, 2, Q, TILE), i16),
             pltpu.VMEM((2, 2, Q, TILE), i16),
             dma,
-            dma((4, 2)),
+            dma((4, 2, W // B)),
             dma, dma,
             dma((3,)), dma((4,)), dma((3,)), dma((8,)), dma((4,)),
             dma((2, 2, 8)), dma((2, 2, 8)), dma((8, 2)), dma((8, 2)),

time: 50.5 us -> 50.6 us (level)
  no operation moved by 1% of the time
where the time goes in v5:
time: 50.6 us; the launch traced here: 50.5 us
  Pallas kernels  49.8 us (98%)
  local copies, waits for them, and re-layouts  0.71 us (1%)
    pallas_call x1, Pallas kernels, body(): pl.pallas_call(kernel, out_shape=jax.ShapeDtypeStruct((TILE, K), f32), in...  49.8 us

profile of v5, /device:TPU:2, one launch (start us, length us, event | category | flops | bytes accessed | tf_op | source)
XLA Modules:
  0.0 50.5 jit_solution(18178469962050966615)
XLA Ops:
  0.0 49.8 %group_z.1 = f32[256,256]{1,0:T(8,128)S(1)} custom-call(f32[300,1,8192]{2,1,0:T(1,128)} %bitcast.2, s32[1,256]{1,0:T(1,128)} %bitcast.3), custom_call_target="tpu_custom_call" | custom-call | tf_op jit(solution)/shard_map/group_z/pallas_call | solution.py:502
  49.8 0.7 %copy.4 = f32[256,256]{1,0:T(8,128)} copy(f32[256,256]{1,0:T(8,128)S(1)} %group_z.1) | data formatting | bytes 524288
